TPU v7x, 32 devices: a whole 2x2x4 slice. The times are simulated.
32 devices in a mesh: seq: 16 (over z, y, x), tp: 2 (over core).
Axes of the slice: x: 2, y: 2, z: 4, core: 2. Of those that a mesh axis runs over, the one named last changes fastest.
Arguments:
- inner_input: bfloat16 [4096, 2560], P('seq', 'tp'), may hold values from -6 to 6
- gate_input: bfloat16 [4096, 2560], P('seq', 'tp'), may hold values from -170 to 170
- state_input: bfloat16 [4096, 256], P('seq'), may hold values from -6 to 6
- step_raw: float32 [40, 4096], P('tp', 'seq'), may hold values from -14 to 0
- conv_inner: float32 [4, 2560], P(None, 'tp'), may hold values from -3 to 3
- conv_state: float32 [4, 256], replicated, may hold values from -3 to 3
- bias_inner: float32 [2560], P('tp'), may hold values from -3 to 3
- bias_state: float32 [256], replicated, may hold values from -3 to 3
- step_bias: float32 [40], P('tp'), may hold values from -0.3 to 0.3
- decay_log: float32 [40], P('tp'), may hold values from -1.4 to 0
- skip_gain: float32 [40], P('tp'), may hold values from 0.5 to 1.5
- norm_gain: float32 [2560], P('tp'), may hold values from 0.1 to 1.9
- out_weight: bfloat16 [2560, 2560], P('tp'), may hold values from -0.15625 to 0.15625
Outputs:
- block_out: bfloat16 [4096, 2560], P('seq', 'tp')
All inputs are finite; a program needn't handle non-finite values.
Results may differ from a plain program's by a relative error of at most 0.008.
Values may be sent and summed in bfloat16 or wider, within the bound.
A program may use at most 64 MiB of HBM per device.

v0:
```python
import jax
import jax.numpy as jnp
from jax import lax
from jax.sharding import PartitionSpec as P

HEAD_DIM = 64
NSTATE = 128
INNER = 2560


highest = lax.Precision.HIGHEST


def passed_along(value, axis, steps):
    count = lax.axis_size(axis)
    leading, last = (max(0, -steps), min(count, count - steps))
    return lax.ppermute(value, axis, [(source, source + steps) for source in range(leading, last)])


def conv_silu(padded, weights, offsets, length):
    width_taps = weights.shape[0]
    summed = offsets[None, :] + jnp.zeros((length, weights.shape[1]), jnp.float32)
    for number in range(width_taps):
        summed = summed + weights[number][None, :] * padded[number : number + length]
    return jax.nn.silu(summed).astype(jnp.bfloat16)


def block_pass(inner_rows, keys_b, query_c, step_sizes, log_decay, state_now):
    cumulative = jnp.cumsum(log_decay, axis=1)
    block_rows = log_decay.shape[1]
    causal = jnp.arange(block_rows)[:, None] >= jnp.arange(block_rows)[None, :]
    spread = jnp.where(causal[None], cumulative[:, :, None] - cumulative[:, None, :], -jnp.inf)
    scores = jnp.dot(query_c, keys_b.T, preferred_element_type=jnp.float32)
    weights = scores[None] * jnp.exp(spread) * step_sizes[:, None, :]
    output = jnp.einsum("hts,shp->thp", weights, inner_rows, precision=highest)
    query_float = query_c.astype(jnp.float32)
    carried = jnp.einsum("tn,hnp->thp", query_float, state_now, precision=highest)
    output = output + carried * jnp.exp(cumulative).T[:, :, None]
    towards_end = jnp.exp(cumulative[:, -1:] - cumulative) * step_sizes
    update = jnp.einsum(
        "sn,shp->hnp",
        keys_b.astype(jnp.float32),
        inner_rows * towards_end.T[:, :, None],
        precision=highest,
    )
    state_next = jnp.exp(cumulative[:, -1])[:, None, None] * state_now + update
    return (state_next, output)


def combine_rows(earlier, later):
    return (earlier[0] * later[0], later[0][..., None] * earlier[1] + later[1])


def local(
    inner_input,
    gate_input,
    state_input,
    step_raw,
    conv_inner,
    conv_state,
    bias_inner,
    bias_state,
    step_bias,
    decay_log,
    skip_gain,
    norm_gain,
    out_weight,
):
    width_taps = conv_inner.shape[0]
    tok_rows = inner_input.shape[0]
    head_count = step_raw.shape[0]
    rims = passed_along(
        (inner_input[tok_rows - width_taps + 1 :], state_input[tok_rows - width_taps + 1 :]),
        "seq",
        1,
    )
    inner_conv = conv_silu(
        jnp.concatenate([rims[0], inner_input], axis=0).astype(jnp.float32),
        conv_inner,
        bias_inner,
        tok_rows,
    )
    state_conv = conv_silu(
        jnp.concatenate([rims[1], state_input], axis=0).astype(jnp.float32),
        conv_state,
        bias_state,
        tok_rows,
    )
    step_sizes = jax.nn.softplus(step_raw + step_bias[:, None])
    log_decay = -jnp.exp(decay_log)[:, None] * step_sizes
    inner_float = inner_conv.astype(jnp.float32).reshape(tok_rows, head_count, HEAD_DIM)
    keys_b = state_conv[:, :NSTATE]
    query_c = state_conv[:, NSTATE:]
    state_now = jnp.zeros((head_count, NSTATE, HEAD_DIM), jnp.float32)
    state_now, output = block_pass(inner_float, keys_b, query_c, step_sizes, log_decay, state_now)
    device_decay = jnp.exp(jnp.sum(log_decay, axis=1))
    devices = lax.axis_size("seq")
    slice_cols = NSTATE * HEAD_DIM // devices
    sliced = state_now.reshape(head_count, devices, slice_cols)
    received = lax.all_to_all(sliced, "seq", split_axis=1, concat_axis=1, tiled=True)
    all_decays = lax.all_gather(device_decay[None, :], "seq", axis=0, tiled=True)
    by_source = jnp.transpose(received, (1, 0, 2))
    running_prefix = lax.associative_scan(combine_rows, (all_decays, by_source), axis=0)
    exclusive = jnp.concatenate([jnp.zeros_like(by_source[:1]), running_prefix[1][:-1]], axis=0)
    returned = lax.all_to_all(
        jnp.transpose(exclusive, (1, 0, 2)), "seq", split_axis=1, concat_axis=1, tiled=True
    )
    entering_state = returned.reshape(head_count, NSTATE, HEAD_DIM)
    cumulative = jnp.cumsum(log_decay, axis=1)
    carried = jnp.einsum(
        "tn,hnp->thp", query_c.astype(jnp.float32), entering_state, precision=highest
    )
    mixed = (
        output
        + carried * jnp.exp(cumulative).T[:, :, None]
        + skip_gain[None, :, None] * inner_float
    )
    gated_raw = mixed.reshape(tok_rows, head_count * HEAD_DIM) * jax.nn.silu(
        gate_input.astype(jnp.float32)
    )
    local_squares = jnp.sum(gated_raw * gated_raw, axis=1)
    gated = (gated_raw * norm_gain[None, :]).astype(jnp.bfloat16)
    partial_out = jnp.dot(gated, out_weight, preferred_element_type=jnp.float32)
    squares = lax.psum(local_squares, "tp")
    summed = lax.psum_scatter(partial_out, "tp", scatter_dimension=1, tiled=True)
    scale_inv = lax.rsqrt(squares / INNER + 1e-05)
    return (summed * scale_inv[:, None]).astype(jnp.bfloat16)


def solution(mesh):
    return jax.shard_map(
        local,
        mesh=mesh,
        in_specs=(
            P("seq", "tp"),
            P("seq", "tp"),
            P("seq", None),
            P("tp", "seq"),
            P(None, "tp"),
            P(),
            P("tp"),
            P(),
            P("tp"),
            P("tp"),
            P("tp"),
            P("tp"),
            P("tp", None),
        ),
        out_specs=P("seq", "tp"),
        check_vma=False,
    )
```

profile of v0, /device:TPU:9, one launch (start us, length us, event | category | flops | bytes accessed | tf_op | source)
XLA Modules:
  0.0 130.0 jit_solution(17599040376568187160)
XLA Ops:
  6.5 0.8 slice.170
  7.3 3.1 %collective-permute-start.1 = (bf16[3,256]{1,0:T(4,128)(2,1)S(1)}, bf16[3,256]{1,0:T(4,128)(2,1)S(1)}, u32[]{:S(2)}, u32[]{:S(2)}) collective-permute-start(bf16[3,256]{1,0:T(4,128)(2,1)S(1)} %slice.170), channel_id=1, source_target_pairs={{0,2},{2,4},{4,6},{6,8},{8,10},{10,12},{12,14},{14,16},{16,18},{18... | collective-permute-start | bytes 4616 | tf_op jit(solution)/shard_map/ppermute | solution.py:17
  10.4 0.7 slice.161
  11.1 3.1 %collective-permute-start = (bf16[3,1280]{1,0:T(4,128)(2,1)S(1)}, bf16[3,1280]{1,0:T(4,128)(2,1)S(1)}, u32[]{:S(2)}, u32[]{:S(2)}) collective-permute-start(bf16[3,1280]{1,0:T(4,128)(2,1)S(1)} %slice.161), channel_id=1, source_target_pairs={{0,2},{2,4},{4,6},{6,8},{8,10},{10,12},{12,14},{14,16},{16,18},{18... | collective-permute-start | bytes 23048 | tf_op jit(solution)/shard_map/ppermute | solution.py:17
  14.3 0.7 exponential_negate_fusion
  14.9 0.8 fusion.63
  15.8 0.9 fusion.60
  16.7 0.6 reduce-window.6
  18.0 0.9 slice_reduce_fusion.5
  18.9 0.9 maximum_convert_fusion.1
  19.9 0.9 multiply_convert_fusion.4
  20.9 0.8 multiply_convert_fusion.2
  22.0 0.8 fusion.34
  22.8 0.4 copy.36
  23.5 1.3 copy.37
  24.8 5.7 %all-to-all-start = ((f32[20,16,512]{2,0,1:T(8,128)}), f32[20,16,512]{2,0,1:T(8,128)S(1)}, u32[]{:S(2)}, u32[]{:S(2)}) async-start(f32[20,16,512]{2,0,1:T(8,128)} %copy.37), calls=%async_computation | async-start | bytes 1572864 | tf_op jit(solution)/shard_map/all_to_all | solution.py:100
  30.5 0.6 dynamic-slice
  31.9 34.7 %all-reduce.9 = f32[320]{0:T(512)S(1)} all-reduce(f32[320]{0:T(512)S(1)} %exponential_dynamic-update-slice_fusion), channel_id=2, replica_groups=mesh['seq'=16,'tp'=2] {'seq'}, use_global_device_ids=true, to_apply=%add.9 | all-reduce | flops 320 | bytes 2560
  68.2 1.0 pad_bitcast_fusion
  69.2 6.9 %all-to-all-start.1 = ((f32[20,16,512]{2,0,1:T(8,128)}), f32[20,16,512]{2,0,1:T(8,128)S(1)}, u32[]{:S(2)}, u32[]{:S(2)}) async-start(f32[20,16,512]{2,0,1:T(8,128)} %pad_bitcast_fusion), calls=%async_computation.1 | async-start | bytes 1572864 | tf_op jit(solution)/shard_map/all_to_all | solution.py:105
  76.4 0.9 fusion.48
  77.3 1.7 %fusion.39 = f32[256,1280]{0,1} fusion(bf16[256,256]{1,0:T(8,128)(2,1)S(1)} %multiply_convert_fusion.4), kind=kOutput, calls=%fused_computation.48 | convolution fusion | flops 503316480 | bytes 1376256
  79.1 9.3 %all-to-all-done.1 = f32[20,16,512]{2,0,1:T(8,128)S(1)} async-done(((f32[20,16,512]{2,0,1:T(8,128)}), f32[20,16,512]{2,0,1:T(8,128)S(1)}, u32[]{:S(2)}, u32[]{:S(2)}) %all-to-all-start.1) | async-done | bytes 655392 | tf_op jit(solution)/shard_map/all_to_all | solution.py:105
  89.5 0.7 fusion.50
  90.2 0.6 copy-done
  90.8 4.0 %fusion.21 = f32[256,20,64]{0,2,1:T(8,128)S(1)} fusion(bf16[256,20,64]{0,2,1:T(8,128)(2,1)S(1)} %bitcast.47, f32[20,256]{1,0:T(8,128)S(1)} %get-tuple-element.11, f32[20,256]{1,0:T(8,128)S(1)} %bitcast.54, f32[256,256]{1,0:T(8,128)S(1)} %copy-done.3, pred[256,256]{1,0:T(8,128)(4,1)S(1)} %iota_compare_fusion, f32[256,20,64]{0,2,1:T(8,128)S(1)} %bitcast.51, ...), kind=kOutput, calls=%fused_computation.19 | convolution fusion | flops 1014169600 | bytes 4976720 | tf_op jit(solution)/shard_map/hts,shp->thp/dot_general | solution.py:35
  95.2 0.7 copy-done.2
  95.9 6.3 %fusion.35 = f32[256,2560]{1,0:T(8,128)} fusion(bf16[1280,2560]{1,0:T(8,128)(2,1)} %param.25, f32[1280]{0:T(1024)S(1)} %copy-done.5, f32[256,1280]{1,0:T(8,128)S(1)} %copy.40, bf16[256,1280]{1,0:T(8,128)(2,1)S(1)} %copy-done.2), kind=kOutput, calls=%fused_computation.41 | convolution fusion | flops 1680343040 | bytes 11146240 | tf_op jit(solution)/shard_map/dot_general | solution.py:123
  102.2 0.5 multiply_reduce_fusion
  102.7 11.7 %psum.7 = f32[256]{0:T(256)S(1)} all-reduce(f32[256]{0:T(256)S(1)} %multiply_reduce_fusion), channel_id=1, replica_groups=mesh['seq'=16,'tp'=2] {'tp'}, use_global_device_ids=true, to_apply=%region_5.6 | all-reduce | flops 256 | bytes 2048 | tf_op jit(solution)/shard_map/psum | solution.py:124
  114.5 6.4 %reduce-scatter.2.cloned.1.call-done = f32[256,1280]{1,0:T(8,128)} async-done(((f32[256,2560]{1,0:T(8,128)}), f32[256,1280]{1,0:T(8,128)}) %reduce-scatter.2.cloned.1.call-update) | async-done | bytes 1310736 | tf_op jit(solution)/shard_map/reduce_scatter | solution.py:125
  120.9 2.3 %multiply_convert_fusion = bf16[256,1280]{1,0:T(8,128)(2,1)} fusion(f32[256,1280]{1,0:T(8,128)} %reduce-scatter.2.cloned.1.call-done, f32[256]{0:T(256)S(1)} %add_rsqrt_fusion), kind=kLoop, calls=%fused_computation.33 | loop fusion | flops 655360 | bytes 1967104 | tf_op jit(solution)/shard_map/convert_element_type | solution.py:127
  (78 shorter events, 4.7 us)
Async XLA Ops:
  6.5 14.2 %copy-start.1 = (bf16[256,1280]{1,0:T(8,128)(2,1)S(1)}, bf16[256,1280]{1,0:T(8,128)(2,1)}, u32[]{:S(2)}) copy-start(bf16[256,1280]{1,0:T(8,128)(2,1)} %param.13) | copy-start | bytes 1966084
  7.3 11.6 %collective-permute-start.1 = (bf16[3,256]{1,0:T(4,128)(2,1)S(1)}, bf16[3,256]{1,0:T(4,128)(2,1)S(1)}, u32[]{:S(2)}, u32[]{:S(2)}) collective-permute-start(bf16[3,256]{1,0:T(4,128)(2,1)S(1)} %slice.170), channel_id=1, source_target_pairs={{0,2},{2,4},{4,6},{6,8},{8,10},{10,12},{12,14},{14,16},{16,18},{18... | collective-permute-start | bytes 4616 | tf_op jit(solution)/shard_map/ppermute | solution.py:17
  11.1 9.6 %collective-permute-start = (bf16[3,1280]{1,0:T(4,128)(2,1)S(1)}, bf16[3,1280]{1,0:T(4,128)(2,1)S(1)}, u32[]{:S(2)}, u32[]{:S(2)}) collective-permute-start(bf16[3,1280]{1,0:T(4,128)(2,1)S(1)} %slice.161), channel_id=1, source_target_pairs={{0,2},{2,4},{4,6},{6,8},{8,10},{10,12},{12,14},{14,16},{16,18},{18... | collective-permute-start | bytes 23048 | tf_op jit(solution)/shard_map/ppermute | solution.py:17
  19.8 1.0 copy-start.4
  23.5 7.0 %copy-start.7 = (u32[32]{0:T(128)S(1)}, u32[32]{0:T(128)}, u32[]{:S(2)}) copy-start(u32[32]{0:T(128)} %constant.43) | copy-start | bytes 388
  24.8 42.0 %all-to-all-start = ((f32[20,16,512]{2,0,1:T(8,128)}), f32[20,16,512]{2,0,1:T(8,128)S(1)}, u32[]{:S(2)}, u32[]{:S(2)}) async-start(f32[20,16,512]{2,0,1:T(8,128)} %copy.37), calls=%async_computation | async-start | bytes 1572864 | tf_op jit(solution)/shard_map/all_to_all | solution.py:100
  69.2 19.2 %all-to-all-start.1 = ((f32[20,16,512]{2,0,1:T(8,128)}), f32[20,16,512]{2,0,1:T(8,128)S(1)}, u32[]{:S(2)}, u32[]{:S(2)}) async-start(f32[20,16,512]{2,0,1:T(8,128)} %pad_bitcast_fusion), calls=%async_computation.1 | async-start | bytes 1572864 | tf_op jit(solution)/shard_map/all_to_all | solution.py:105
  76.2 44.7 %reduce-scatter.2.cloned.1.call-start = ((), (), s32[]{:S(2)}) async-start(), calls=%async_computation.3 | async-start | bytes 3932160 | tf_op jit(solution)/shard_map/reduce_scatter | solution.py:125
  89.4 1.3 %copy-start = (f32[256,1280]{0,1:S(1)}, f32[256,1280]{0,1}, u32[]{:S(2)}) copy-start(f32[256,1280]{0,1} %fusion.39) | copy-start | bytes 3932164
  89.4 1.3 %copy-start.3 = (f32[256,256]{1,0:T(8,128)S(1)}, f32[256,256]{1,0:T(8,128)}, u32[]{:S(2)}) copy-start(f32[256,256]{1,0:T(8,128)} %fusion.48) | copy-start | bytes 786436
  89.5 1.3 %copy-start.6 = (f32[20]{0:T(128)S(1)}, f32[20]{0:T(128)}, u32[]{:S(2)}) copy-start(f32[20]{0:T(128)} %param.23) | copy-start | bytes 244
  94.8 1.1 copy-start.2
  94.8 1.1 copy-start.5
Sparse Core Ops, SparseCore 0:
  102.3 18.5 reduce-scatter.1
where the time goes:
time: 132 us; the launch traced here: 130 us
  blocking collectives  46.4 us (35%)
  starting transfers between devices  19.1 us (14%)
  waiting for transfers between devices  15.8 us (12%)
  between operations  14.5 us (11%)
  matrix products  14.4 us (11%)
  local copies, waits for them, and re-layouts  11 us (8%)
  other arithmetic  8.9 us (7%)
    unnamed x1, blocking collectives  34.7 us
    psum x1, blocking collectives, local(): squares = lax.psum(local_squares, 'tp')  11.7 us
    all_to_all x1, waiting for transfers between devices, local(): lax.all_to_all(jnp.transpose(exclusive, (1, 0, 2)), 'seq', split_axis=1,...  9.34 us
    all_to_all x1, starting transfers between devices, local(): lax.all_to_all(jnp.transpose(exclusive, (1, 0, 2)), 'seq', split_axis=1,...  6.93 us
    reduce_scatter x1, waiting for transfers between devices, local(): lax.psum_scatter(partial_out, 'tp', scatter_dimension=1, tiled=True)  6.44 us
    dot_general x1, matrix products, local(): partial_out = jnp.dot(gated, out_weight, preferred_element_type=jnp.float32)  6.31 us
    ppermute x2, starting transfers between devices, passed_along(): lax.ppermute(value, axis, [(source, source + steps) for source in range(l...  6.21 us
    all_to_all x1, starting transfers between devices, local(): lax.all_to_all(sliced, 'seq', split_axis=1, concat_axis=1, tiled=True)  5.71 us
  transfers between devices with their start and end apart: 5, of which 2 were waited for; matrix products, arithmetic and copies ran while one was open for 9% of the time, Pallas kernels for 0%

commit v1 on v0

v1 whole, which is shorter than its diff:
```python
import functools

import jax
import jax.numpy as jnp
from jax import lax
from jax.experimental import pallas as pl
from jax.experimental.pallas import tpu as pltpu
from jax.sharding import PartitionSpec as P

HEAD_DIM = 64
NSTATE = 128
LANES = 128
GROUP = 32
RIM = 8
MESH = pl.DeviceIdType.MESH
f32 = jnp.float32
bf16 = jnp.bfloat16


def silu(v):
    return v / (1.0 + jnp.exp(-v))


def log1p_exp(v):
    u = jnp.exp(-jnp.abs(v))
    z = u / (2.0 + u)
    q = z * z
    series = jnp.full_like(q, 1.0 / 19.0)
    for odd in range(17, 0, -2):
        series = series * q + 1.0 / odd
    return jnp.maximum(v, 0.0) + 2.0 * z * series


def spread_heads(table, ones):
    high = table.astype(bf16)
    low = (table - high.astype(f32)).astype(bf16)
    out = jnp.dot(high, ones, preferred_element_type=f32)
    return out + jnp.dot(low, ones, preferred_element_type=f32)


def conv_rows(src, taps, bias, start, rows, columns):
    count = taps.shape[0]
    total = bias[...]
    for k in range(count):
        first = start + RIM - count + 1 + k
        total = total + taps[k : k + 1] * src[pl.ds(first, rows), columns]
    return silu(total)


def kernel(
    n,
    x_hbm, gate_hbm, state_in, step_raw, taps_x, taps_s, bias_x, bias_s,
    step_bias, decay_log, skip_gain, norm_gain, w_hbm,
    out_ref,
    x_in, gate_in, w_all, x_pad, s_pad, x_conv, s_conv, table, spread, cols,
    scores, mixed, gate_act, decayed, gated,
    rim_x, rim_s, decay_out, decay_all, decay_cols,
    full, slices, got1, back, got2, entering,
    part, part_got, own, squares, squares_got,
    load_sem, rim_send, rim_recv, d_send, d_recv, s1_send, s1_recv,
    s2_send, s2_recv, o_send, o_recv, q_sem,
):
    me = lax.axis_index("seq")
    core = lax.axis_index("tp")
    other = 1 - core
    rows, inner = x_in.shape
    heads = step_raw.shape[0]
    tiles = inner // LANES
    per = NSTATE // n
    slot = slices.shape[1]
    half = rows // 2

    barrier = pltpu.get_barrier_semaphore()

    def greet(k, _):
        pl.semaphore_signal(
            barrier, inc=1, device_id={"seq": lax.rem(me + k, n)}, device_id_type=MESH
        )
        return 0

    lax.fori_loop(1, n, greet, 0)
    pl.semaphore_signal(barrier, inc=1, device_id={"tp": other}, device_id_type=MESH)

    load_x = pltpu.make_async_copy(x_hbm, x_in, load_sem.at[0])
    load_g = pltpu.make_async_copy(gate_hbm, gate_in, load_sem.at[1])
    load_w = pltpu.make_async_copy(w_hbm, w_all, load_sem.at[2])
    load_x.start()
    load_g.start()
    load_w.start()

    eye = (
        lax.broadcasted_iota(jnp.int32, (heads, heads), 0)
        == lax.broadcasted_iota(jnp.int32, (heads, heads), 1)
    )

    def as_column(row):
        return jnp.sum(jnp.where(eye, row[...], 0.0), axis=1, keepdims=True)

    step = log1p_exp(step_raw[...] + as_column(step_bias))
    log_decay = -jnp.exp(as_column(decay_log)) * step
    upper = (
        lax.broadcasted_iota(jnp.int32, (rows, rows), 0)
        <= lax.broadcasted_iota(jnp.int32, (rows, rows), 1)
    ).astype(f32)
    cum = jnp.dot(
        log_decay, upper, precision=lax.Precision.HIGHEST, preferred_element_type=f32
    )
    shifted = cum - jnp.log(step)
    table[...] = jnp.zeros_like(table)
    table[0:heads] = cum
    table[GROUP : GROUP + heads] = jnp.exp(cum[:, rows - 1 : rows] - shifted)
    table[2 * GROUP : 2 * GROUP + heads] = jnp.exp(cum)
    flipped = table[...].T
    cols[...] = flipped
    lane = lax.broadcasted_iota(jnp.int32, (1, LANES), 1) // GROUP
    decay_out[...] = jnp.where(
        lane == 2, jnp.broadcast_to(flipped[rows - 1 : rows], (8, LANES)), 0.0
    )
    decay_all[me] = decay_out[...]

    pl.semaphore_wait(barrier, n)

    def rim_copies():
        target = {"seq": lax.rem(me + 1, n)}
        return [
            pltpu.make_async_remote_copy(
                src_ref=src.at[pl.ds(rows - RIM, RIM)],
                dst_ref=dst,
                send_sem=rim_send.at[i],
                recv_sem=rim_recv.at[i],
                device_id=target,
                device_id_type=MESH,
            )
            for i, (src, dst) in enumerate(((x_hbm, rim_x), (state_in, rim_s)))
        ]

    @pl.when(me < n - 1)
    def _():
        for copy in rim_copies():
            copy.start()

    def decay_copy(k):
        to = lax.rem(me + k, n)
        return pltpu.make_async_remote_copy(
            src_ref=decay_out,
            dst_ref=decay_all.at[me],
            send_sem=d_send.at[k],
            recv_sem=d_recv.at[me],
            device_id={"seq": to},
            device_id_type=MESH,
        )

    def decay_start(k, _):
        decay_copy(k).start()
        return 0

    lax.fori_loop(1, n, decay_start, 0)

    spread[...] = jnp.where(
        lax.broadcasted_iota(jnp.int32, (LANES, inner), 0) % GROUP
        == lax.broadcasted_iota(jnp.int32, (LANES, inner), 1) // HEAD_DIM,
        1.0,
        0.0,
    ).astype(bf16)

    s_pad[0:RIM] = jnp.zeros((RIM, s_pad.shape[1]), f32)
    s_pad[RIM:] = state_in[...].astype(f32)
    s_conv[...] = conv_rows(s_pad, taps_s, bias_s, 0, rows, slice(None)).astype(bf16)
    x_pad[0:RIM] = jnp.zeros((RIM, inner), f32)
    load_x.wait()
    for i in range(tiles):
        c = slice(i * LANES, (i + 1) * LANES)
        x_pad[RIM:, c] = x_in[:, c].astype(f32)
        x_conv[:, c] = conv_rows(
            x_pad, taps_x[:, c], bias_x[:, c], 0, rows, c
        ).astype(bf16)

    @pl.when(me > 0)
    def _():
        for copy in rim_copies():
            copy.wait_recv()
        s_pad[0:RIM] = rim_s[...].astype(f32)
        x_pad[0:RIM] = rim_x[...].astype(f32)

    s_conv[0:16] = conv_rows(s_pad, taps_s, bias_s, 0, 16, slice(None)).astype(bf16)
    x_conv[0:16] = conv_rows(x_pad, taps_x, bias_x, 0, 16, slice(None)).astype(bf16)

    towards = jnp.where(lane == 1, cols[...], 0.0)
    for i in range(tiles):
        c = slice(i * LANES, (i + 1) * LANES)
        scaled = (
            x_conv[:, c].astype(f32) * spread_heads(towards, spread[:, c])
        ).astype(bf16)
        full[:, c] = lax.dot_general(
            s_conv[:, :NSTATE], scaled, (((0,), (0,)), ((), ())),
            preferred_element_type=f32,
        )

    def cut(j, _):
        piece = full[pl.ds(pl.multiple_of(j * per, per), per), :]
        slices[j] = jnp.broadcast_to(piece, (slot, inner)).astype(bf16)
        return 0

    lax.fori_loop(0, n, cut, 0)

    def state_copy(k):
        to = lax.rem(me + k, n)
        return pltpu.make_async_remote_copy(
            src_ref=slices.at[to],
            dst_ref=got1.at[me],
            send_sem=s1_send.at[k],
            recv_sem=s1_recv.at[me],
            device_id={"seq": to},
            device_id_type=MESH,
        )

    @pl.when(me < n - 1)
    def _():
        def start(k, _):
            state_copy(k).start()
            return 0

        lax.fori_loop(1, n, start, 0)

    got1[me] = slices[me]

    def decay_wait(k, _):
        source = lax.rem(me + k, n)
        pltpu.make_async_remote_copy(
            src_ref=decay_out,
            dst_ref=decay_all.at[source],
            send_sem=d_send.at[k],
            recv_sem=d_recv.at[source],
            device_id={"seq": source},
            device_id_type=MESH,
        ).wait_recv()
        return 0

    lax.fori_loop(1, n, decay_wait, 0)
    decay_cols[...] = spread_heads(
        decay_all[...].reshape(n * 8, LANES), spread[...]
    ).reshape(n, 8, inner)

    keys = s_conv[:, :NSTATE]
    query = s_conv[:, NSTATE:]
    causal = (
        lax.broadcasted_iota(jnp.int32, (rows, rows), 0)
        >= lax.broadcasted_iota(jnp.int32, (rows, rows), 1)
    )
    scores[...] = jnp.where(
        causal,
        lax.dot_general(
            query, keys, (((1,), (1,)), ((), ())), preferred_element_type=f32
        ),
        0.0,
    )
    first_half = lax.broadcasted_iota(jnp.int32, (1, LANES), 1) < HEAD_DIM

    def inside(i):
        c = slice(i * LANES, (i + 1) * LANES)
        x_c = x_conv[:, c]
        tops, bottoms = [], []
        for h in (2 * i, 2 * i + 1):
            a_row = shifted[h : h + 1, :]
            top = cols[0:half, h : h + 1] - a_row[:, :half]
            top = scores[0:half, 0:half] * jnp.exp(jnp.minimum(top, 80.0))
            tops.append(
                jnp.dot(top.astype(bf16), x_c[:half], preferred_element_type=f32)
            )
            low = cols[half:, h : h + 1] - a_row
            low = scores[half:, :] * jnp.exp(jnp.minimum(low, 80.0))
            bottoms.append(jnp.dot(low.astype(bf16), x_c, preferred_element_type=f32))
        gain = jnp.where(
            first_half,
            skip_gain[:, 2 * i : 2 * i + 1],
            skip_gain[:, 2 * i + 1 : 2 * i + 2],
        )
        x_f = x_c.astype(f32)
        mixed[0:half, c] = jnp.where(first_half, *tops) + gain * x_f[:half]
        mixed[half:, c] = jnp.where(first_half, *bottoms) + gain * x_f[half:]

    split = (tiles * 6) // 10
    for i in range(split):
        inside(i)

    state = jnp.zeros((slot, inner), f32)

    def prefix(j, state):
        back[j] = state.astype(bf16)

        @pl.when(j != me)
        def _():
            pltpu.make_async_remote_copy(
                src_ref=slices.at[j],
                dst_ref=got1.at[j],
                send_sem=s1_send.at[0],
                recv_sem=s1_recv.at[j],
                device_id={"seq": lax.rem(me + 1, n)},
                device_id_type=MESH,
            ).wait_recv()

        return decay_cols[j][0:1] * state + got1[j].astype(f32)

    state = lax.fori_loop(0, n - 1, prefix, state)
    back[n - 1] = state.astype(bf16)

    def back_copy(k):
        to = lax.rem(me + k, n)
        return to, pltpu.make_async_remote_copy(
            src_ref=back.at[to],
            dst_ref=got2.at[me],
            send_sem=s2_send.at[k],
            recv_sem=s2_recv.at[me],
            device_id={"seq": to},
            device_id_type=MESH,
        )

    def back_start(k, _):
        to, copy = back_copy(k)

        @pl.when(to > 0)
        def _():
            copy.start()

        return 0

    lax.fori_loop(1, n, back_start, 0)
    got2[me] = back[me]

    for i in range(split, tiles):
        inside(i)

    load_g.wait()
    carry_decay = jnp.where(lane == 2, cols[...], 0.0)
    for i in range(tiles):
        c = slice(i * LANES, (i + 1) * LANES)
        gate_act[:, c] = silu(gate_in[:, c].astype(f32))
        decayed[:, c] = spread_heads(carry_decay, spread[:, c])

    @pl.when(me > 0)
    def _():
        def back_wait(k, _):
            source = lax.rem(me + k, n)
            pltpu.make_async_remote_copy(
                src_ref=back.at[source],
                dst_ref=got2.at[source],
                send_sem=s2_send.at[k],
                recv_sem=s2_recv.at[source],
                device_id={"seq": source},
                device_id_type=MESH,
            ).wait_recv()
            return 0

        lax.fori_loop(1, n, back_wait, 0)

        def place(j, _):
            entering[pl.ds(pl.multiple_of(j * per, per), per), :] = got2[j].astype(
                f32
            )[0:per]
            return 0

        lax.fori_loop(0, n, place, 0)

    @pl.when(me == 0)
    def _():
        entering[...] = jnp.zeros_like(entering)

    total = jnp.zeros((rows, LANES), f32)
    for i in range(tiles):
        c = slice(i * LANES, (i + 1) * LANES)
        carried = jnp.dot(
            query, entering[:, c].astype(bf16), preferred_element_type=f32
        )
        raw = (mixed[:, c] + carried * decayed[:, c]) * gate_act[:, c]
        total = total + raw * raw
        gated[:, c] = (raw * norm_gain[:, c]).astype(bf16)
    squares[...] = total

    def across(src, dst, send, recv):
        return pltpu.make_async_remote_copy(
            src_ref=src,
            dst_ref=dst,
            send_sem=send,
            recv_sem=recv,
            device_id={"tp": other},
            device_id_type=MESH,
        )

    copy_q = across(squares, squares_got, q_sem.at[0], q_sem.at[1])
    copy_q.start()
    load_w.wait()
    pieces, _, width = part.shape

    def part_copy(p):
        return across(part.at[p], part_got.at[p], o_send.at[p], o_recv.at[p])

    for p in range(pieces):
        at = pl.ds(pl.multiple_of(other * inner + p * width, LANES), width)
        part[p] = jnp.dot(
            gated[...], w_all[:, at], preferred_element_type=f32
        ).astype(bf16)
        part_copy(p).start()
    for p in range(pieces):
        at = pl.ds(pl.multiple_of(core * inner + p * width, LANES), width)
        own[p] = jnp.dot(gated[...], w_all[:, at], preferred_element_type=f32)
    copy_q.wait_recv()
    both = jnp.sum(squares[...] + squares_got[...], axis=1, keepdims=True)
    scale = lax.rsqrt(both / (2 * inner) + 1e-05)
    for p in range(pieces):
        part_copy(p).wait_recv()
        out_ref[:, p * width : (p + 1) * width] = (
            (own[p] + part_got[p].astype(f32)) * scale
        ).astype(bf16)

    copy_q.wait_send()
    for p in range(pieces):
        part_copy(p).wait_send()

    def drain(k, _):
        decay_copy(k).wait_send()
        to, copy = back_copy(k)

        @pl.when(to > 0)
        def _():
            copy.wait_send()

        return 0

    lax.fori_loop(1, n, drain, 0)

    @pl.when(me < n - 1)
    def _():
        for copy in rim_copies():
            copy.wait_send()

        def drain1(k, _):
            state_copy(k).wait_send()
            return 0

        lax.fori_loop(1, n, drain1, 0)


def local(
    inner_input, gate_input, state_input, step_raw, conv_inner, conv_state,
    bias_inner, bias_state, step_bias, decay_log, skip_gain, norm_gain, out_weight,
):
    n = lax.axis_size("seq")
    rows, inner = inner_input.shape
    maps = state_input.shape[1]
    slot = max(8, NSTATE // n)
    width = 256
    pieces = inner // width
    vm = pltpu.VMEM
    dma = pltpu.SemaphoreType.DMA
    any_spec = pl.BlockSpec(memory_space=pl.ANY)
    vmem_spec = pl.BlockSpec(memory_space=pltpu.VMEM)
    scratch = [
        vm((rows, inner), bf16),
        vm((rows, inner), bf16),
        vm(out_weight.shape, bf16),
        vm((rows + RIM, inner), f32),
        vm((rows + RIM, maps), f32),
        vm((rows, inner), bf16),
        vm((rows, maps), bf16),
        vm((LANES, rows), f32),
        vm((LANES, inner), bf16),
        vm((rows, LANES), f32),
        vm((rows, rows), f32),
        vm((rows, inner), f32),
        vm((rows, inner), f32),
        vm((rows, inner), f32),
        vm((rows, inner), bf16),
        vm((RIM, inner), bf16),
        vm((RIM, maps), bf16),
        vm((8, LANES), f32),
        vm((n, 8, LANES), f32),
        vm((n, 8, inner), f32),
        vm((NSTATE, inner), f32),
        vm((n, slot, inner), bf16),
        vm((n, slot, inner), bf16),
        vm((n, slot, inner), bf16),
        vm((n, slot, inner), bf16),
        vm((NSTATE, inner), f32),
        vm((pieces, rows, width), bf16),
        vm((pieces, rows, width), bf16),
        vm((pieces, rows, width), f32),
        vm((rows, LANES), f32),
        vm((rows, LANES), f32),
        dma((3,)), dma((2,)), dma((2,)),
        dma((n,)), dma((n,)), dma((n,)), dma((n,)), dma((n,)), dma((n,)),
        dma((pieces,)), dma((pieces,)), dma((2,)),
    ]
    row = lambda v: v.reshape(1, -1)
    return pl.pallas_call(
        functools.partial(kernel, n),
        out_shape=jax.ShapeDtypeStruct((rows, inner), bf16),
        in_specs=[any_spec, any_spec] + [vmem_spec] * 10 + [any_spec],
        out_specs=vmem_spec,
        scratch_shapes=scratch,
        compiler_params=pltpu.CompilerParams(
            collective_id=0, has_side_effects=True, vmem_limit_bytes=60 * 2**20
        ),
        name="ssd_block",
    )(
        inner_input, gate_input, state_input, step_raw, conv_inner, conv_state,
        row(bias_inner), row(bias_state), row(step_bias), row(decay_log),
        row(skip_gain), row(norm_gain), out_weight,
    )


def solution(mesh):
    return jax.shard_map(
        local,
        mesh=mesh,
        in_specs=(
            P("seq", "tp"),
            P("seq", "tp"),
            P("seq", None),
            P("tp", "seq"),
            P(None, "tp"),
            P(),
            P("tp"),
            P(),
            P("tp"),
            P("tp"),
            P("tp"),
            P("tp"),
            P("tp", None),
        ),
        out_specs=P("seq", "tp"),
        check_vma=False,
    )
```

time: 132 us -> 41.3 us (0.31); the launches traced: 130 us -> 41.1 us
  blocking collectives: 46.4 us -> 0 us
  Pallas kernels: 0 us -> 36.5 us
  starting transfers between devices: 19.1 us -> 0 us
  waiting for transfers between devices: 15.8 us -> 0 us
  between operations: 14.5 us -> 0.01 us
  matrix products: 14.4 us -> 0 us
  other arithmetic: 8.9 us -> 0 us
  local copies, waits for them, and re-layouts: 11 us -> 4.53 us
    pallas_call x0 -> x1, Pallas kernels: none -> 36.5 us  [local(): pl.pallas_call(functools.partial(kernel, n), out_shape=jax.ShapeDtypeStru...]
    unnamed x1 -> x0, blocking collectives: 34.7 us -> none
    all_to_all x2 -> x0, starting transfers between devices: 12.6 us -> none  [the longest x1 6.93 us: local(): lax.all_to_all(jnp.transpose(exclusive, (1, 0, 2)), 'seq', split_axis=1,...]
    dot_general x4 -> x0, matrix products: 12 us -> none  [the longest x1 6.31 us: local(): partial_out = jnp.dot(gated, out_weight, preferred_element_type=jnp.float32)]
    psum x1 -> x0, blocking collectives: 11.7 us -> none  [local(): squares = lax.psum(local_squares, 'tp')]
    all_to_all x2 -> x0, waiting for transfers between devices: 9.34 us -> none  [the longest x1 9.34 us: local(): lax.all_to_all(jnp.transpose(exclusive, (1, 0, 2)), 'seq', split_axis=1,...]
    reduce_scatter x1 -> x0, waiting for transfers between devices: 6.44 us -> none  [local(): lax.psum_scatter(partial_out, 'tp', scatter_dimension=1, tiled=True)]
    ppermute x2 -> x0, starting transfers between devices: 6.21 us -> none  [passed_along(): lax.ppermute(value, axis, [(source, source + steps) for source in range(l...]
  transfers between devices with their start and end apart: 5 -> 0, of which waited for: 2 -> 0; matrix products, arithmetic and copies ran while one was open for 9% -> 0% of each run, Pallas kernels for 0% -> 0%
where the time goes in v1:
time: 41.3 us; the launch traced here: 41.1 us
  Pallas kernels  36.5 us (88%)
  local copies, waits for them, and re-layouts  4.53 us (11%)
    pallas_call x1, Pallas kernels, local(): pl.pallas_call(functools.partial(kernel, n), out_shape=jax.ShapeDtypeStru...  36.5 us
    reshape x2, local copies, waits for them, and re-layouts, local(): row = lambda v: v.reshape(1, -1)  2.57 us
    unnamed x1, local copies, waits for them, and re-layouts  1.97 us

profile of v1, /device:TPU:9, one launch (start us, length us, event | category | flops | bytes accessed | tf_op | source)
XLA Modules:
  0.0 41.1 jit_solution(1446219442246310377)
XLA Ops:
  0.0 1.3 %reshape.18.bias_x = f32[1,1280]{1,0:T(1,128)} reshape(f32[1280]{0:T(1024)} %param.19) | data formatting | bytes 10240 | tf_op jit(solution)/shard_map/reshape | solution.py:493
  1.3 1.3 %reshape.23.norm_gain = f32[1,1280]{1,0:T(1,128)} reshape(f32[1280]{0:T(1024)} %param.24) | data formatting | bytes 10240 | tf_op jit(solution)/shard_map/reshape | solution.py:493
  2.6 36.5 %ssd_block.1 = bf16[256,1280]{1,0:T(8,128)(2,1)} custom-call(bf16[256,1280]{1,0:T(8,128)(2,1)} %x_hbm.1, bf16[256,1280]{1,0:T(8,128)(2,1)} %gate_hbm.1, bf16[256,256]{1,0:T(8,128)(2,1)} %state_in.1, f32[20,256]{1,0:T(8,128)} %step_raw.1, f32[4,1280]{1,0:T(4,128)} %taps_x.1, f32[4,256]{1,0:T(4,128)} %taps_s.1, f32[1,1280]{1,0:T(1,128)} %reshape.18.bias_x, ...), custom_call_target="tpu_custom_call" | custom-call | tf_op jit(solution)/shard_map/ssd_block/pallas_call | solution.py:494
  39.1 2.0 %copy.15 = bf16[256,1280]{1,0:T(8,128)(2,1)} copy(bf16[256,1280]{1,0:T(8,128)(2,1)} %ssd_block.1) | data formatting | bytes 1310720

commit v2 on v1

--- a/solution.py
+++ b/solution.py
@@ -118,8 +118,6 @@
     )
     decay_all[me] = decay_out[...]
 
-    pl.semaphore_wait(barrier, n)
-
     def rim_copies():
         target = {"seq": lax.rem(me + 1, n)}
         return [
@@ -134,6 +132,27 @@
             for i, (src, dst) in enumerate(((x_hbm, rim_x), (state_in, rim_s)))
         ]
 
+    spread[...] = jnp.where(
+        lax.broadcasted_iota(jnp.int32, (LANES, inner), 0) % GROUP
+        == lax.broadcasted_iota(jnp.int32, (LANES, inner), 1) // HEAD_DIM,
+        1.0,
+        0.0,
+    ).astype(bf16)
+
+    s_pad[0:RIM] = jnp.zeros((RIM, s_pad.shape[1]), f32)
+    s_pad[RIM:] = state_in[...].astype(f32)
+    s_conv[...] = conv_rows(s_pad, taps_s, bias_s, 0, rows, slice(None)).astype(bf16)
+    x_pad[0:RIM] = jnp.zeros((RIM, inner), f32)
+    load_x.wait()
+    for i in range(tiles):
+        c = slice(i * LANES, (i + 1) * LANES)
+        x_pad[RIM:, c] = x_in[:, c].astype(f32)
+        x_conv[:, c] = conv_rows(
+            x_pad, taps_x[:, c], bias_x[i : i + 1], 0, rows, c
+        ).astype(bf16)
+
+    pl.semaphore_wait(barrier, n)
+
     @pl.when(me < n - 1)
     def _():
         for copy in rim_copies():
@@ -156,24 +175,12 @@
 
     lax.fori_loop(1, n, decay_start, 0)
 
-    spread[...] = jnp.where(
-        lax.broadcasted_iota(jnp.int32, (LANES, inner), 0) % GROUP
-        == lax.broadcasted_iota(jnp.int32, (LANES, inner), 1) // HEAD_DIM,
-        1.0,
-        0.0,
-    ).astype(bf16)
-
-    s_pad[0:RIM] = jnp.zeros((RIM, s_pad.shape[1]), f32)
-    s_pad[RIM:] = state_in[...].astype(f32)
-    s_conv[...] = conv_rows(s_pad, taps_s, bias_s, 0, rows, slice(None)).astype(bf16)
-    x_pad[0:RIM] = jnp.zeros((RIM, inner), f32)
-    load_x.wait()
+    load_g.wait()
+    carry_decay = jnp.where(lane == 2, cols[...], 0.0)
     for i in range(tiles):
         c = slice(i * LANES, (i + 1) * LANES)
-        x_pad[RIM:, c] = x_in[:, c].astype(f32)
-        x_conv[:, c] = conv_rows(
-            x_pad, taps_x[:, c], bias_x[:, c], 0, rows, c
-        ).astype(bf16)
+        gate_act[:, c] = silu(gate_in[:, c].astype(f32))
+        decayed[:, c] = spread_heads(carry_decay, spread[:, c])
 
     @pl.when(me > 0)
     def _():
@@ -183,7 +190,11 @@
         x_pad[0:RIM] = rim_x[...].astype(f32)
 
     s_conv[0:16] = conv_rows(s_pad, taps_s, bias_s, 0, 16, slice(None)).astype(bf16)
-    x_conv[0:16] = conv_rows(x_pad, taps_x, bias_x, 0, 16, slice(None)).astype(bf16)
+    for i in range(tiles):
+        c = slice(i * LANES, (i + 1) * LANES)
+        x_conv[0:16, c] = conv_rows(
+            x_pad, taps_x[:, c], bias_x[i : i + 1], 0, 16, c
+        ).astype(bf16)
 
     towards = jnp.where(lane == 1, cols[...], 0.0)
     for i in range(tiles):
@@ -330,13 +341,6 @@
     for i in range(split, tiles):
         inside(i)
 
-    load_g.wait()
-    carry_decay = jnp.where(lane == 2, cols[...], 0.0)
-    for i in range(tiles):
-        c = slice(i * LANES, (i + 1) * LANES)
-        gate_act[:, c] = silu(gate_in[:, c].astype(f32))
-        decayed[:, c] = spread_heads(carry_decay, spread[:, c])
-
     @pl.when(me > 0)
     def _():
         def back_wait(k, _):
@@ -373,7 +377,7 @@
         )
         raw = (mixed[:, c] + carried * decayed[:, c]) * gate_act[:, c]
         total = total + raw * raw
-        gated[:, c] = (raw * norm_gain[:, c]).astype(bf16)
+        gated[:, c] = (raw * norm_gain[i : i + 1]).astype(bf16)
     squares[...] = total
 
     def across(src, dst, send, recv):
@@ -452,7 +456,7 @@
     pieces = inner // width
     vm = pltpu.VMEM
     dma = pltpu.SemaphoreType.DMA
-    any_spec = pl.BlockSpec(memory_space=pl.ANY)
+    any_spec = pl.BlockSpec(memory_space=pltpu.HBM)
     vmem_spec = pl.BlockSpec(memory_space=pltpu.VMEM)
     scratch = [
         vm((rows, inner), bf16),
@@ -491,6 +495,7 @@
         dma((pieces,)), dma((pieces,)), dma((2,)),
     ]
     row = lambda v: v.reshape(1, -1)
+    tile = lambda v: v.reshape(-1, LANES)
     return pl.pallas_call(
         functools.partial(kernel, n),
         out_shape=jax.ShapeDtypeStruct((rows, inner), bf16),
@@ -498,13 +503,13 @@
         out_specs=vmem_spec,
         scratch_shapes=scratch,
         compiler_params=pltpu.CompilerParams(
-            collective_id=0, has_side_effects=True, vmem_limit_bytes=60 * 2**20
+            collective_id=0, has_side_effects=True, vmem_limit_bytes=58 * 2**20
         ),
         name="ssd_block",
     )(
         inner_input, gate_input, state_input, step_raw, conv_inner, conv_state,
-        row(bias_inner), row(bias_state), row(step_bias), row(decay_log),
-        row(skip_gain), row(norm_gain), out_weight,
+        tile(bias_inner), row(bias_state), row(step_bias), row(decay_log),
+        row(skip_gain), tile(norm_gain), out_weight,
     )
 
 

time: 41.3 us -> 38.2 us (0.925)
  local copies, waits for them, and re-layouts: 4.53 us -> 1.97 us
    reshape x2 -> x0, local copies, waits for them, and re-layouts: 2.57 us -> none  [local(): row = lambda v: v.reshape(1, -1)]
    pallas_call x1, Pallas kernels: 36.5 us -> 36.1 us  [local(): pl.pallas_call(functools.partial(kernel, n), out_shape=jax.ShapeDtypeStru...]
where the time goes in v2:
time: 38.2 us; the launch traced here: 38 us
  Pallas kernels  36.1 us (95%)
  local copies, waits for them, and re-layouts  1.97 us (5%)
    pallas_call x1, Pallas kernels, local(): pl.pallas_call(functools.partial(kernel, n), out_shape=jax.ShapeDtypeStru...  36.1 us
    unnamed x1, local copies, waits for them, and re-layouts  1.97 us

profile of v2, /device:TPU:9, one launch (start us, length us, event | category | flops | bytes accessed | tf_op | source)
XLA Modules:
  0.0 38.0 jit_solution(12589624050505020327)
XLA Ops:
  0.0 36.1 %ssd_block.1 = bf16[256,1280]{1,0:T(8,128)(2,1)} custom-call(bf16[256,1280]{1,0:T(8,128)(2,1)} %x_hbm.1, bf16[256,1280]{1,0:T(8,128)(2,1)} %gate_hbm.1, bf16[256,256]{1,0:T(8,128)(2,1)} %state_in.1, f32[20,256]{1,0:T(8,128)} %step_raw.1, f32[4,1280]{1,0:T(4,128)} %taps_x.1, f32[4,256]{1,0:T(4,128)} %taps_s.1, f32[10,128]{1,0:T(8,128)} %bitcast.6, ...), custom_call_target="tpu_custom_call" | custom-call | tf_op jit(solution)/shard_map/ssd_block/pallas_call | solution.py:499
  36.1 2.0 %copy.15 = bf16[256,1280]{1,0:T(8,128)(2,1)} copy(bf16[256,1280]{1,0:T(8,128)(2,1)} %ssd_block.1) | data formatting | bytes 1310720

commit v3 on v2

--- a/solution.py
+++ b/solution.py
@@ -67,7 +67,8 @@
     heads = step_raw.shape[0]
     tiles = inner // LANES
     per = NSTATE // n
-    slot = slices.shape[1]
+    slot = slices.shape[2]
+    wide = inner // 2
     half = rows // 2
 
     barrier = pltpu.get_barrier_semaphore()
@@ -196,44 +197,47 @@
             x_pad, taps_x[:, c], bias_x[i : i + 1], 0, 16, c
         ).astype(bf16)
 
-    towards = jnp.where(lane == 1, cols[...], 0.0)
-    for i in range(tiles):
-        c = slice(i * LANES, (i + 1) * LANES)
-        scaled = (
-            x_conv[:, c].astype(f32) * spread_heads(towards, spread[:, c])
-        ).astype(bf16)
-        full[:, c] = lax.dot_general(
-            s_conv[:, :NSTATE], scaled, (((0,), (0,)), ((), ())),
-            preferred_element_type=f32,
-        )
-
-    def cut(j, _):
-        piece = full[pl.ds(pl.multiple_of(j * per, per), per), :]
-        slices[j] = jnp.broadcast_to(piece, (slot, inner)).astype(bf16)
-        return 0
-
-    lax.fori_loop(0, n, cut, 0)
-
-    def state_copy(k):
+    def state_copy(part_no, k):
         to = lax.rem(me + k, n)
         return pltpu.make_async_remote_copy(
-            src_ref=slices.at[to],
-            dst_ref=got1.at[me],
-            send_sem=s1_send.at[k],
-            recv_sem=s1_recv.at[me],
+            src_ref=slices.at[part_no, to],
+            dst_ref=got1.at[part_no, me],
+            send_sem=s1_send.at[part_no, k],
+            recv_sem=s1_recv.at[part_no, me],
             device_id={"seq": to},
             device_id_type=MESH,
         )
 
-    @pl.when(me < n - 1)
-    def _():
-        def start(k, _):
-            state_copy(k).start()
+    towards = jnp.where(lane == 1, cols[...], 0.0)
+    for b in range(2):
+        for i in range(b * tiles // 2, (b + 1) * tiles // 2):
+            c = slice(i * LANES, (i + 1) * LANES)
+            scaled = (
+                x_conv[:, c].astype(f32) * spread_heads(towards, spread[:, c])
+            ).astype(bf16)
+            full[:, c] = lax.dot_general(
+                s_conv[:, :NSTATE], scaled, (((0,), (0,)), ((), ())),
+                preferred_element_type=f32,
+            )
+
+        def cut(j, _, b=b):
+            piece = full[
+                pl.ds(pl.multiple_of(j * per, per), per), b * wide : (b + 1) * wide
+            ]
+            slices[b, j] = jnp.broadcast_to(piece, (slot, wide)).astype(bf16)
             return 0
 
-        lax.fori_loop(1, n, start, 0)
-
-    got1[me] = slices[me]
+        lax.fori_loop(0, n, cut, 0)
+
+        @pl.when(me < n - 1)
+        def _(b=b):
+            def start(k, _):
+                state_copy(b, k).start()
+                return 0
+
+            lax.fori_loop(1, n, start, 0)
+
+        got1[b, me] = slices[b, me]
 
     def decay_wait(k, _):
         source = lax.rem(me + k, n)
@@ -290,80 +294,79 @@
         mixed[0:half, c] = jnp.where(first_half, *tops) + gain * x_f[:half]
         mixed[half:, c] = jnp.where(first_half, *bottoms) + gain * x_f[half:]
 
-    split = (tiles * 6) // 10
-    for i in range(split):
+    for i in range(tiles):
         inside(i)
 
-    state = jnp.zeros((slot, inner), f32)
-
-    def prefix(j, state):
-        back[j] = state.astype(bf16)
-
-        @pl.when(j != me)
-        def _():
-            pltpu.make_async_remote_copy(
-                src_ref=slices.at[j],
-                dst_ref=got1.at[j],
-                send_sem=s1_send.at[0],
-                recv_sem=s1_recv.at[j],
-                device_id={"seq": lax.rem(me + 1, n)},
-                device_id_type=MESH,
-            ).wait_recv()
-
-        return decay_cols[j][0:1] * state + got1[j].astype(f32)
-
-    state = lax.fori_loop(0, n - 1, prefix, state)
-    back[n - 1] = state.astype(bf16)
-
-    def back_copy(k):
+    def back_copy(b, k):
         to = lax.rem(me + k, n)
         return to, pltpu.make_async_remote_copy(
-            src_ref=back.at[to],
-            dst_ref=got2.at[me],
-            send_sem=s2_send.at[k],
-            recv_sem=s2_recv.at[me],
+            src_ref=back.at[b, to],
+            dst_ref=got2.at[b, me],
+            send_sem=s2_send.at[b, k],
+            recv_sem=s2_recv.at[b, me],
             device_id={"seq": to},
             device_id_type=MESH,
         )
 
-    def back_start(k, _):
-        to, copy = back_copy(k)
-
-        @pl.when(to > 0)
-        def _():
-            copy.start()
-
-        return 0
-
-    lax.fori_loop(1, n, back_start, 0)
-    got2[me] = back[me]
-
-    for i in range(split, tiles):
-        inside(i)
+    for b in range(2):
+        c = slice(b * wide, (b + 1) * wide)
+
+        def prefix(j, state, b=b, c=c):
+            back[b, j] = state.astype(bf16)
+
+            @pl.when(j != me)
+            def _():
+                pltpu.make_async_remote_copy(
+                    src_ref=slices.at[b, j],
+                    dst_ref=got1.at[b, j],
+                    send_sem=s1_send.at[b, 0],
+                    recv_sem=s1_recv.at[b, j],
+                    device_id={"seq": lax.rem(me + 1, n)},
+                    device_id_type=MESH,
+                ).wait_recv()
+
+            return decay_cols[j][0:1, c] * state + got1[b, j].astype(f32)
+
+        state = lax.fori_loop(0, n - 1, prefix, jnp.zeros((slot, wide), f32))
+        back[b, n - 1] = state.astype(bf16)
+
+        def back_start(k, _, b=b):
+            to, copy = back_copy(b, k)
+
+            @pl.when(to > 0)
+            def _():
+                copy.start()
+
+            return 0
+
+        lax.fori_loop(1, n, back_start, 0)
+        got2[b, me] = back[b, me]
 
     @pl.when(me > 0)
     def _():
-        def back_wait(k, _):
-            source = lax.rem(me + k, n)
-            pltpu.make_async_remote_copy(
-                src_ref=back.at[source],
-                dst_ref=got2.at[source],
-                send_sem=s2_send.at[k],
-                recv_sem=s2_recv.at[source],
-                device_id={"seq": source},
-                device_id_type=MESH,
-            ).wait_recv()
-            return 0
-
-        lax.fori_loop(1, n, back_wait, 0)
-
-        def place(j, _):
-            entering[pl.ds(pl.multiple_of(j * per, per), per), :] = got2[j].astype(
-                f32
-            )[0:per]
-            return 0
-
-        lax.fori_loop(0, n, place, 0)
+        for b in range(2):
+
+            def back_wait(k, _, b=b):
+                source = lax.rem(me + k, n)
+                pltpu.make_async_remote_copy(
+                    src_ref=back.at[b, source],
+                    dst_ref=got2.at[b, source],
+                    send_sem=s2_send.at[b, k],
+                    recv_sem=s2_recv.at[b, source],
+                    device_id={"seq": source},
+                    device_id_type=MESH,
+                ).wait_recv()
+                return 0
+
+            lax.fori_loop(1, n, back_wait, 0)
+
+            def place(j, _, b=b):
+                entering[
+                    pl.ds(pl.multiple_of(j * per, per), per), b * wide : (b + 1) * wide
+                ] = got2[b, j].astype(f32)[0:per]
+                return 0
+
+            lax.fori_loop(0, n, place, 0)
 
     @pl.when(me == 0)
     def _():
@@ -422,11 +425,12 @@
 
     def drain(k, _):
         decay_copy(k).wait_send()
-        to, copy = back_copy(k)
-
-        @pl.when(to > 0)
-        def _():
-            copy.wait_send()
+        for b in range(2):
+            to, copy = back_copy(b, k)
+
+            @pl.when(to > 0)
+            def _(copy=copy):
+                copy.wait_send()
 
         return 0
 
@@ -438,7 +442,8 @@
             copy.wait_send()
 
         def drain1(k, _):
-            state_copy(k).wait_send()
+            state_copy(0, k).wait_send()
+            state_copy(1, k).wait_send()
             return 0
 
         lax.fori_loop(1, n, drain1, 0)
@@ -480,10 +485,10 @@
         vm((n, 8, LANES), f32),
         vm((n, 8, inner), f32),
         vm((NSTATE, inner), f32),
-        vm((n, slot, inner), bf16),
-        vm((n, slot, inner), bf16),
-        vm((n, slot, inner), bf16),
-        vm((n, slot, inner), bf16),
+        vm((2, n, slot, inner // 2), bf16),
+        vm((2, n, slot, inner // 2), bf16),
+        vm((2, n, slot, inner // 2), bf16),
+        vm((2, n, slot, inner // 2), bf16),
         vm((NSTATE, inner), f32),
         vm((pieces, rows, width), bf16),
         vm((pieces, rows, width), bf16),
@@ -491,7 +496,7 @@
         vm((rows, LANES), f32),
         vm((rows, LANES), f32),
         dma((3,)), dma((2,)), dma((2,)),
-        dma((n,)), dma((n,)), dma((n,)), dma((n,)), dma((n,)), dma((n,)),
+        dma((n,)), dma((n,)), dma((2, n)), dma((2, n)), dma((2, n)), dma((2, n)),
         dma((pieces,)), dma((pieces,)), dma((2,)),
     ]
     row = lambda v: v.reshape(1, -1)

time: 38.2 us -> 37 us (0.969); the launches traced: 38 us -> 36.4 us
  Pallas kernels: 36.1 us -> 34.4 us
    pallas_call x1, Pallas kernels: 36.1 us -> 34.4 us  [local(): pl.pallas_call(functools.partial(kernel, n), out_shape=jax.ShapeDtypeStru...]
where the time goes in v3:
time: 37 us; the launch traced here: 36.4 us
  Pallas kernels  34.4 us (93%)
  local copies, waits for them, and re-layouts  1.97 us (5%)
    pallas_call x1, Pallas kernels, local(): pl.pallas_call(functools.partial(kernel, n), out_shape=jax.ShapeDtypeStru...  34.4 us
    unnamed x1, local copies, waits for them, and re-layouts  1.97 us

profile of v3, /device:TPU:9, one launch (start us, length us, event | category | flops | bytes accessed | tf_op | source)
XLA Modules:
  0.0 36.4 jit_solution(908819315538650668)
XLA Ops:
  0.0 34.4 %ssd_block.1 = bf16[256,1280]{1,0:T(8,128)(2,1)} custom-call(bf16[256,1280]{1,0:T(8,128)(2,1)} %x_hbm.1, bf16[256,1280]{1,0:T(8,128)(2,1)} %gate_hbm.1, bf16[256,256]{1,0:T(8,128)(2,1)} %state_in.1, f32[20,256]{1,0:T(8,128)} %step_raw.1, f32[4,1280]{1,0:T(4,128)} %taps_x.1, f32[4,256]{1,0:T(4,128)} %taps_s.1, f32[10,128]{1,0:T(8,128)} %bitcast.6, ...), custom_call_target="tpu_custom_call" | custom-call | tf_op jit(solution)/shard_map/ssd_block/pallas_call | solution.py:504
  34.4 2.0 %copy.15 = bf16[256,1280]{1,0:T(8,128)(2,1)} copy(bf16[256,1280]{1,0:T(8,128)(2,1)} %ssd_block.1) | data formatting | bytes 1310720
